TPU v7x, 128 devices: a whole 4x4x4 slice. The times are simulated.
128 devices in a mesh: expert: 8 (over y, core), mp: 16 (over z, x).
Axes of the slice: x: 4, y: 4, z: 4, core: 2. Of those that a mesh axis runs over, the one named last changes fastest.
Arguments:
- tokens: bfloat16 [2048, 6144], P(('expert', 'mp')), may hold values from -18 to 18
- norm_gain: bfloat16 [6144], replicated, may hold values from 0.099609375 to 1.8984375
- expert_ids: int32 [2048, 2], P(('expert', 'mp')), may hold values from 0 to 7, as said below
- slot_ids: int32 [2048, 2], P(('expert', 'mp')), may hold values from 0 to 7, as said below
- route_weights: float32 [2048, 2], P(('expert', 'mp')), may hold values from 0.1 to 1
- w_gate: bfloat16 [8, 6144, 8192], P('expert', None, 'mp'), may hold values from -0.078125 to 0.078125
- w_up: bfloat16 [8, 6144, 8192], P('expert', None, 'mp'), may hold values from -0.078125 to 0.078125
- w_down: bfloat16 [8, 8192, 6144], P('expert', 'mp'), may hold values from -0.0625 to 0.0625
Outputs:
- moe_out: bfloat16 [2048, 6144], P(('expert', 'mp'))
Inputs may be any that keep to these rules, and one draw needn't show every extreme that they name: `expert_ids`: each token names two different experts. Among the 16 tokens of one device (aligned blocks of rows) no expert is named more than 8 times, and on every device some expert is named exactly 8 times. `slot_ids`: within the tokens of one device, the entries that name the same expert have different slots; slots that no entry names stay empty.
All inputs are finite; a program needn't handle non-finite values.
Results may differ from a plain program's by a relative error of at most 0.015.
Values may be sent and summed in bfloat16 or wider, within the bound.
A program may use at most 128 MiB of HBM per device.

v0:
```python
import jax
import jax.numpy as jnp
from jax import lax
from jax.sharding import PartitionSpec as P

CAP = 8


def local(tokens, norm_gain, expert_ids, slot_ids, route_weights, w_gate, w_up, w_down):
    tok_rows = tokens.shape[0]
    features = tokens.shape[1]
    experts = w_gate.shape[0] * lax.axis_size("expert")
    values = tokens.astype(jnp.float32)
    mean_square = jnp.mean(values * values, axis=1, keepdims=True)
    normed = (values * lax.rsqrt(mean_square + 1e-05) * norm_gain.astype(jnp.float32)).astype(
        jnp.bfloat16
    )
    target = expert_ids * CAP + slot_ids
    places = lax.broadcasted_iota(jnp.int32, (experts * CAP, tok_rows, 2), 0)
    placing = jnp.any(places == target[None, :, :], axis=2).astype(jnp.bfloat16)
    outgoing = jnp.dot(placing, normed, preferred_element_type=jnp.float32).astype(jnp.bfloat16)
    outgoing = outgoing.reshape(experts, CAP, features)
    gate_local = w_gate[0]
    up_local = w_up[0]
    down_local = w_down[0]
    arrived = lax.all_to_all(outgoing, "expert", split_axis=0, concat_axis=0, tiled=True)
    piece = lax.all_gather(arrived.reshape(experts * CAP, features), "mp", axis=0, tiled=True)
    gate_proj = jnp.dot(piece, gate_local, preferred_element_type=jnp.float32)
    up_proj = jnp.dot(piece, up_local, preferred_element_type=jnp.float32)
    hidden = (jax.nn.silu(gate_proj) * up_proj).astype(jnp.bfloat16)
    piece = hidden
    summed = lax.psum_scatter(
        jnp.dot(piece, down_local, preferred_element_type=jnp.float32).astype(jnp.bfloat16),
        "mp",
        scatter_dimension=0,
        tiled=True,
    )
    results = summed.reshape(experts, CAP, features)
    returned = lax.all_to_all(results, "expert", split_axis=0, concat_axis=0, tiled=True)
    flattened = returned.reshape(experts * CAP, features)
    picked = flattened[target].astype(jnp.float32)
    shares = route_weights / (route_weights[:, 0:1] + route_weights[:, 1:2])
    mixed = jnp.sum(shares[:, :, None] * picked, axis=1)
    return mixed.astype(jnp.bfloat16)


def solution(mesh):
    placed = (
        P(("expert", "mp"), None),
        P(),
        P(("expert", "mp"), None),
        P(("expert", "mp"), None),
        P(("expert", "mp"), None),
        P("expert", None, "mp"),
        P("expert", None, "mp"),
        P("expert", "mp", None),
    )
    return jax.shard_map(
        local, mesh=mesh, in_specs=placed, out_specs=P(("expert", "mp"), None), check_vma=False
    )
```

profile of v0, /device:TPU:1, one launch (start us, length us, event | category | flops | bytes accessed | tf_op | source)
XLA Modules:
  0.0 274.3 jit_solution(11265923259628819744)
XLA Ops:
  6.5 0.0 all-gather.2.cloned.1.call-start
  6.5 0.7 compare_select_fusion
  7.2 0.1 fusion.14
  7.3 0.7 convert_element_type.26
  8.0 1.1 fusion.8
  9.1 1.3 fusion
  10.5 18.0 %all_to_all.10 = bf16[8,8,6144]{2,1,0:T(8,128)(2,1)} all-to-all(bf16[8,8,6144]{2,1,0:T(8,128)(2,1)S(1)} %fusion), channel_id=1, replica_groups=mesh['expert'=8,'mp'=16] {'expert'}, dimensions={0} | all-to-all | bytes 1572864 | tf_op jit(solution)/shard_map/all_to_all | solution.py:26
  28.5 0.0 all-gather.2.cloned.1.call-update
  28.5 0.0 reduce-scatter.2.cloned.1.call-start
  28.5 90.6 %all-gather.2.cloned.1.call-done = bf16[1024,6144]{1,0:T(8,128)(2,1)} async-done(((bf16[64,6144]{1,0:T(8,128)(2,1)}), bf16[1024,6144]{1,0:T(8,128)(2,1)}) %all-gather.2.cloned.1.call-update) | async-done | bytes 12582928 | tf_op jit(solution)/shard_map/all_gather | solution.py:27
  119.1 0.0 copy-start.1
  119.1 11.6 %fusion.2 = f32[1024,512]{1,0:T(8,128)S(1)} fusion(bf16[1024,6144]{1,0:T(8,128)(2,1)} %all-gather.2.cloned.1.call-done, bf16[1,6144,512]{2,1,0:T(8,128)(2,1)} %param.14), kind=kOutput, calls=%fused_computation.5 | convolution fusion | flops 6442450944 | bytes 20971520 | tf_op jit(solution)/shard_map/dot_general | solution.py:29
  130.7 0.0 copy-done.1
  130.7 8.9 %multiply_convert_fusion = bf16[1024,512]{1,0:T(8,128)(2,1)S(1)} fusion(f32[1024,512]{1,0:T(8,128)S(1)} %fusion.2, bf16[1024,6144]{1,0:T(8,128)(2,1)S(1)} %copy-done.1, bf16[1,6144,512]{2,1,0:T(8,128)(2,1)} %param.13), kind=kOutput, calls=%fused_computation.9 | convolution fusion | flops 6445596672 | bytes 22020096 | tf_op jit(solution)/shard_map/dot_general | solution.py:28
  139.7 12.4 %convolution_convert_fusion = bf16[1024,6144]{1,0:T(8,128)(2,1)} fusion(bf16[1024,512]{1,0:T(8,128)(2,1)S(1)} %multiply_convert_fusion, bf16[1,512,6144]{2,1,0:T(8,128)(2,1)} %param.15), kind=kOutput, calls=%fused_computation.1 | convolution fusion | flops 6448742400 | bytes 19922944 | tf_op jit(solution)/shard_map/dot_general | solution.py:33
  152.0 0.0 copy-start
  152.0 0.0 reduce-scatter.2.cloned.1.call-update
  152.0 94.8 %reduce-scatter.2.cloned.1.call-done = bf16[64,6144]{1,0:T(8,128)(2,1)} async-done(((bf16[1024,6144]{1,0:T(8,128)(2,1)}), bf16[64,6144]{1,0:T(8,128)(2,1)}) %reduce-scatter.2.cloned.1.call-update) | async-done | bytes 786448 | tf_op jit(solution)/shard_map/reduce_scatter | solution.py:32
  246.8 5.5 %all-to-all-start.1 = ((bf16[8,8,6144]{2,1,0:T(8,128)(2,1)}), bf16[8,8,6144]{2,1,0:T(8,128)(2,1)S(1)}, u32[]{:S(2)}, u32[]{:S(2)}) async-start(bf16[8,8,6144]{2,1,0:T(8,128)(2,1)} %bitcast.24), calls=%async_computation.2 | async-start | bytes 1572864 | tf_op jit(solution)/shard_map/all_to_all | solution.py:39
  252.3 0.1 copy.16
  252.4 0.1 reshape.29
  252.4 0.0 copy-done
  252.5 0.1 copy.15
  252.6 11.9 %all-to-all-done.1 = bf16[8,8,6144]{2,1,0:T(8,128)(2,1)S(1)} async-done(((bf16[8,8,6144]{2,1,0:T(8,128)(2,1)}), bf16[8,8,6144]{2,1,0:T(8,128)(2,1)S(1)}, u32[]{:S(2)}, u32[]{:S(2)}) %all-to-all-start.1) | async-done | bytes 786464 | tf_op jit(solution)/shard_map/all_to_all | solution.py:39
  264.4 0.8 gather_fusion
  265.2 0.5 reshape.37
  265.7 1.7 multiply_reduce_fusion
  (4 shorter events, 0.0 us)
Async XLA Ops:
  6.5 112.6 %all-gather.2.cloned.1.call-start = ((), (), s32[]{:S(2)}) async-start(), calls=%async_computation.3 | async-start | bytes 13369344 | tf_op jit(solution)/shard_map/all_gather | solution.py:27
  28.5 218.3 %reduce-scatter.2.cloned.1.call-start = ((), (), s32[]{:S(2)}) async-start(), calls=%async_computation.4 | async-start | bytes 13369344 | tf_op jit(solution)/shard_map/reduce_scatter | solution.py:32
  119.1 11.6 %copy-start.1 = (bf16[1024,6144]{1,0:T(8,128)(2,1)S(1)}, bf16[1024,6144]{1,0:T(8,128)(2,1)}, u32[]{:S(2)}) copy-start(bf16[1024,6144]{1,0:T(8,128)(2,1)} %all-gather.2.cloned.1.call-done) | copy-start | bytes 37748740
  152.0 100.4 %copy-start = (f32[16,2]{0,1:T(2,128)S(1)}, f32[16,2]{0,1:T(2,128)}, u32[]{:S(2)}) copy-start(f32[16,2]{0,1:T(2,128)} %param.12) | copy-start | bytes 388
  246.8 17.6 %all-to-all-start.1 = ((bf16[8,8,6144]{2,1,0:T(8,128)(2,1)}), bf16[8,8,6144]{2,1,0:T(8,128)(2,1)S(1)}, u32[]{:S(2)}, u32[]{:S(2)}) async-start(bf16[8,8,6144]{2,1,0:T(8,128)(2,1)} %bitcast.24), calls=%async_computation.2 | async-start | bytes 1572864 | tf_op jit(solution)/shard_map/all_to_all | solution.py:39
Sparse Core Ops, SparseCore 0:
  28.6 90.4 all-gather.1
  152.2 94.6 reduce-scatter.1
where the time goes:
time: 275 us; the launch traced here: 274 us
  waiting for transfers between devices  197 us (72%)
  matrix products  34.2 us (12%)
  blocking collectives  18 us (7%)
  between operations  13.5 us (5%)
  starting transfers between devices  5.5 us (2%)
  other arithmetic  4.34 us (2%)
    reduce_scatter x1, waiting for transfers between devices, local(): lax.psum_scatter(jnp.dot(piece, down_local, preferred_element_type=jnp.fl...  94.8 us
    all_gather x1, waiting for transfers between devices, local(): lax.all_gather(arrived.reshape(experts * CAP, features), 'mp', axis=0, ti...  90.6 us
    all_to_all x1, blocking collectives, local(): lax.all_to_all(outgoing, 'expert', split_axis=0, concat_axis=0, tiled=True)  18 us
    dot_general x1, matrix products, local(): jnp.dot(piece, down_local, preferred_element_type=jnp.float32)  12.4 us
    all_to_all x1, waiting for transfers between devices, local(): lax.all_to_all(results, 'expert', split_axis=0, concat_axis=0, tiled=True)  11.9 us
    dot_general x1, matrix products, local(): up_proj = jnp.dot(piece, up_local, preferred_element_type=jnp.float32)  11.6 us
    dot_general x1, matrix products, local(): gate_proj = jnp.dot(piece, gate_local, preferred_element_type=jnp.float32)  8.94 us
  transfers between devices with their start and end apart: 3, of which 3 were waited for; matrix products, arithmetic and copies ran while one was open for 0% of the time, Pallas kernels for 0%

commit v1 on v0

--- a/solution.py
+++ b/solution.py
@@ -24,7 +24,11 @@
     up_local = w_up[0]
     down_local = w_down[0]
     arrived = lax.all_to_all(outgoing, "expert", split_axis=0, concat_axis=0, tiled=True)
-    piece = lax.all_gather(arrived.reshape(experts * CAP, features), "mp", axis=0, tiled=True)
+    x = arrived.reshape(experts * CAP, features)
+    peers = lax.axis_size("mp")
+    tiles = jnp.stack([x for _ in range(peers)])
+    tiles = lax.all_to_all(tiles, "mp", split_axis=0, concat_axis=0)
+    piece = jnp.concatenate(tiles, axis=0)
     gate_proj = jnp.dot(piece, gate_local, preferred_element_type=jnp.float32)
     up_proj = jnp.dot(piece, up_local, preferred_element_type=jnp.float32)
     hidden = (jax.nn.silu(gate_proj) * up_proj).astype(jnp.bfloat16)

time: 275 us -> 331 us (1.20)
  blocking collectives: 18 us -> 165 us
  waiting for transfers between devices: 197 us -> 104 us
  local copies, waits for them, and re-layouts: 1.54 us -> 7.67 us
  matrix products: 34.2 us -> 30 us
    all_to_all x0 -> x1, blocking collectives: none -> 147 us  [local(): tiles = lax.all_to_all(tiles, 'mp', split_axis=0, concat_axis=0)]
    all_gather x1 -> x0, waiting for transfers between devices: 90.6 us -> none  [local(): lax.all_gather(arrived.reshape(experts * CAP, features), 'mp', axis=0, ti...]
    another operation x0 -> x1, local copies, waits for them, and re-layouts: none -> 6.12 us  [local(): tiles = jnp.stack([x for _ in range(peers)])]
    dot_general x1, matrix products: 11.6 us -> 7.99 us  [local(): up_proj = jnp.dot(piece, up_local, preferred_element_type=jnp.float32)]
  transfers between devices with their start and end apart: 3 -> 2, of which waited for: 3 -> 2; matrix products, arithmetic and copies ran while one was open for 0% -> 0% of each run, Pallas kernels for 0% -> 0%
where the time goes in v1:
time: 331 us; the launch traced here: 330 us
  blocking collectives  165 us (50%)
  waiting for transfers between devices  104 us (31%)
  matrix products  30 us (9%)
  between operations  13.5 us (4%)
  local copies, waits for them, and re-layouts  7.67 us (2%)
  starting transfers between devices  5.46 us (2%)
  other arithmetic  4.34 us (1%)
    all_to_all x1, blocking collectives, local(): tiles = lax.all_to_all(tiles, 'mp', split_axis=0, concat_axis=0)  147 us
    reduce_scatter x1, waiting for transfers between devices, local(): lax.psum_scatter(jnp.dot(piece, down_local, preferred_element_type=jnp.fl...  92 us
    all_to_all x1, blocking collectives, local(): lax.all_to_all(outgoing, 'expert', split_axis=0, concat_axis=0, tiled=True)  17.9 us
    dot_general x1, matrix products, local(): jnp.dot(piece, down_local, preferred_element_type=jnp.float32)  12.4 us
    all_to_all x1, waiting for transfers between devices, local(): lax.all_to_all(results, 'expert', split_axis=0, concat_axis=0, tiled=True)  11.9 us
    dot_general x1, matrix products, local(): gate_proj = jnp.dot(piece, gate_local, preferred_element_type=jnp.float32)  8.36 us
    dot_general x1, matrix products, local(): up_proj = jnp.dot(piece, up_local, preferred_element_type=jnp.float32)  7.99 us
  transfers between devices with their start and end apart: 2, of which 2 were waited for; matrix products, arithmetic and copies ran while one was open for 0% of the time, Pallas kernels for 0%

profile of v1, /device:TPU:1, one launch (start us, length us, event | category | flops | bytes accessed | tf_op | source)
XLA Modules:
  0.0 330.2 jit_solution(12669722394944075678)
XLA Ops:
  6.5 0.0 reduce-scatter.2.cloned.1.call-start
  6.5 0.7 compare_select_fusion
  7.2 0.1 fusion.14
  7.3 0.7 convert_element_type.26
  8.0 1.1 fusion.8
  9.1 1.3 fusion
  10.5 17.9 %all_to_all.15 = bf16[8,8,6144]{2,1,0:T(8,128)(2,1)S(1)} all-to-all(bf16[8,8,6144]{2,1,0:T(8,128)(2,1)S(1)} %fusion), channel_id=1, replica_groups=mesh['expert'=8,'mp'=16] {'expert'}, dimensions={0} | all-to-all | bytes 1572864 | tf_op jit(solution)/shard_map/all_to_all | solution.py:26
  28.4 0.0 slice-start
  28.4 6.1 %stack.3 = bf16[16,64,6144]{2,1,0:T(8,128)(2,1)} broadcast(bf16[64,6144]{1,0:T(8,128)(2,1)S(1)} %bitcast.26), dimensions={1,2} | broadcast | bytes 13369344 | tf_op jit(solution)/shard_map/stack | solution.py:29
  34.5 0.0 slice-start.1
  34.5 0.0 slice-start.2
  34.5 147.4 %all_to_all.16 = bf16[16,64,6144]{2,1,0:T(8,128)(2,1)S(1)} all-to-all(bf16[16,64,6144]{2,1,0:T(8,128)(2,1)} %stack.3), channel_id=1, replica_groups=mesh['expert'=8,'mp'=16] {'mp'}, dimensions={0} | all-to-all | bytes 25165824 | tf_op jit(solution)/shard_map/all_to_all | solution.py:30
  181.9 0.0 slice-done
  181.9 0.0 slice-done.1
  181.9 0.0 slice-start.3
  181.9 8.0 %fusion.2 = f32[1024,512]{1,0:T(8,128)} fusion(bf16[1024,6144]{1,0:T(8,128)(2,1)S(1)} %bitcast.24, bf16[1,6144,512]{2,1,0:T(8,128)(2,1)S(1)} %bitcast.29), kind=kOutput, calls=%fused_computation.5 | convolution fusion | flops 6442450944 | bytes 20971520 | tf_op jit(solution)/shard_map/dot_general | solution.py:33
  189.9 0.0 slice-done.2
  189.9 0.0 slice-done.3
  189.9 8.4 %multiply_convert_fusion = bf16[1024,512]{1,0:T(8,128)(2,1)S(1)} fusion(f32[1024,512]{1,0:T(8,128)} %fusion.2, bf16[1024,6144]{1,0:T(8,128)(2,1)S(1)} %bitcast.25, bf16[1,6144,512]{2,1,0:T(8,128)(2,1)S(1)} %bitcast.31), kind=kOutput, calls=%fused_computation.9 | convolution fusion | flops 6445596672 | bytes 22020096 | tf_op jit(solution)/shard_map/dot_general | solution.py:32
  198.3 12.4 %convolution_convert_fusion = bf16[1024,6144]{1,0:T(8,128)(2,1)} fusion(bf16[1024,512]{1,0:T(8,128)(2,1)S(1)} %multiply_convert_fusion, bf16[1,512,6144]{2,1,0:T(8,128)(2,1)} %param.15), kind=kOutput, calls=%fused_computation.1 | convolution fusion | flops 6448742400 | bytes 19922944 | tf_op jit(solution)/shard_map/dot_general | solution.py:37
  210.6 0.0 copy-start
  210.6 0.0 reduce-scatter.2.cloned.1.call-update
  210.7 92.0 %reduce-scatter.2.cloned.1.call-done = bf16[64,6144]{1,0:T(8,128)(2,1)} async-done(((bf16[1024,6144]{1,0:T(8,128)(2,1)}), bf16[64,6144]{1,0:T(8,128)(2,1)}) %reduce-scatter.2.cloned.1.call-update) | async-done | bytes 786448 | tf_op jit(solution)/shard_map/reduce_scatter | solution.py:36
  302.7 5.5 %all-to-all-start.2 = ((bf16[8,8,6144]{2,1,0:T(8,128)(2,1)}), bf16[8,8,6144]{2,1,0:T(8,128)(2,1)S(1)}, u32[]{:S(2)}, u32[]{:S(2)}) async-start(bf16[8,8,6144]{2,1,0:T(8,128)(2,1)} %bitcast.27), calls=%async_computation.3 | async-start | bytes 1572864 | tf_op jit(solution)/shard_map/all_to_all | solution.py:43
  308.1 0.1 copy.16
  308.2 0.1 reshape.31
  308.3 0.0 copy-done
  308.4 0.1 copy.15
  308.4 11.9 %all-to-all-done.2 = bf16[8,8,6144]{2,1,0:T(8,128)(2,1)S(1)} async-done(((bf16[8,8,6144]{2,1,0:T(8,128)(2,1)}), bf16[8,8,6144]{2,1,0:T(8,128)(2,1)S(1)}, u32[]{:S(2)}, u32[]{:S(2)}) %all-to-all-start.2) | async-done | bytes 786464 | tf_op jit(solution)/shard_map/all_to_all | solution.py:43
  320.3 0.8 gather_fusion
  321.1 0.5 reshape.39
  321.6 1.7 multiply_reduce_fusion
  (6 shorter events, 0.0 us)
Async XLA Ops:
  6.5 296.2 %reduce-scatter.2.cloned.1.call-start = ((), (), s32[]{:S(2)}) async-start(), calls=%async_computation.4 | async-start | bytes 13369344 | tf_op jit(solution)/shard_map/reduce_scatter | solution.py:36
  28.4 153.6 %slice-start = ((s8[6291456]{0:T(1024)(128)(4,1)}), s8[2097152]{0:T(1024)(128)(4,1)S(1)}, s32[]{:S(2)}) async-start(s8[6291456]{0:T(1024)(128)(4,1)} %bitcast.28), calls=%async_computation.5 | async-start | bytes 4194304
  34.5 147.4 %slice-start.1 = ((s8[6291456]{0:T(1024)(128)(4,1)}), s8[4194304]{0:T(1024)(128)(4,1)S(1)}, s32[]{:S(2)}) async-start(s8[6291456]{0:T(1024)(128)(4,1)} %bitcast.28), calls=%async_computation.6 | async-start | bytes 8388608
  34.5 155.4 %slice-start.2 = ((s8[6291456]{0:T(1024)(128)(4,1)}), s8[4194304]{0:T(1024)(128)(4,1)S(1)}, s32[]{:S(2)}) async-start(s8[6291456]{0:T(1024)(128)(4,1)} %bitcast.30), calls=%async_computation.7 | async-start | bytes 8388608
  181.9 8.0 %slice-start.3 = ((s8[6291456]{0:T(1024)(128)(4,1)}), s8[2097152]{0:T(1024)(128)(4,1)S(1)}, s32[]{:S(2)}) async-start(s8[6291456]{0:T(1024)(128)(4,1)} %bitcast.30), calls=%async_computation.8 | async-start | bytes 4194304
  210.6 97.7 %copy-start = (f32[16,2]{0,1:T(2,128)S(1)}, f32[16,2]{0,1:T(2,128)}, u32[]{:S(2)}) copy-start(f32[16,2]{0,1:T(2,128)} %param.12) | copy-start | bytes 388
  302.7 17.6 %all-to-all-start.2 = ((bf16[8,8,6144]{2,1,0:T(8,128)(2,1)}), bf16[8,8,6144]{2,1,0:T(8,128)(2,1)S(1)}, u32[]{:S(2)}, u32[]{:S(2)}) async-start(bf16[8,8,6144]{2,1,0:T(8,128)(2,1)} %bitcast.27), calls=%async_computation.3 | async-start | bytes 1572864 | tf_op jit(solution)/shard_map/all_to_all | solution.py:43
Sparse Core Ops, SparseCore 0:
  210.8 91.8 reduce-scatter.1
